TPU v7x, 32 devices: a whole 2x2x4 slice. The times are simulated.
32 devices in a mesh: ens: 4 (over y, x), slab: 8 (over z, core).
Axes of the slice: x: 2, y: 2, z: 4, core: 2. Of those that a mesh axis runs over, the one named last changes fastest.
Arguments:
- velocity: float32 [4, 3, 8, 2048, 1024], P('ens', None, None, 'slab'), may hold values from -6 to 6
- cutoffs: int32 [4, 2, 8], P('ens'), may hold values from 128 to 511, as said below
- plane_index: int32 [4], P('ens'), may hold values from 0 to 2047
- boundary_index: int32 [4], P('ens'), may hold values from 0 to 2047
Outputs:
- blended: float32 [4, 3, 8, 2048, 1024], P('ens', None, None, 'slab')
Inputs may be any that keep to these rules, and one draw needn't show every extreme that they name: `cutoffs`: row 0 lies in 256 to 511 and row 1 in 128 to 255; in every member some level has row 0 equal to 511 and some level has row 1 equal to 255.
All inputs are finite; a program needn't handle non-finite values.
Results may differ from a plain program's by a relative error of at most 0.0003.
Values sent between devices are 32-bit elements; how exact they have to be, the bound alone decides.
A program may use at most 128 MiB of HBM per device.

v0:
```python
import math
import jax
import jax.numpy as jnp
from jax import lax
from jax.sharding import PartitionSpec as P

KX = 512
KY = 256
highest = lax.Precision.HIGHEST


def spread(value, axis, source):
    kept = jnp.where(lax.axis_index(axis) == source, value, 0).astype(value.dtype)
    return lax.psum(kept, axis)


def shifted(block, axis, distance):
    devices = range(lax.axis_size(axis))
    route = [((i - distance) % len(devices), i) for i in devices]
    return lax.ppermute(block, axis, route)


def basis_pair(length, mode_count):
    position = jnp.arange(length, dtype=jnp.int32)
    wavenum = jnp.arange(mode_count, dtype=jnp.int32)
    angles = (position[:, None] * wavenum[None, :] % length).astype(jnp.float32) * (
        2.0 * math.pi / length
    )
    basis_cols = jnp.concatenate([jnp.cos(angles), jnp.sin(angles)], axis=1)
    weight = jnp.where(wavenum == 0, 1.0, 2.0).astype(jnp.float32) / length
    weight = jnp.concatenate([weight, weight])
    return (basis_cols * weight[None, :], basis_cols.T)


def mode_keep(levels_cut, mode_count):
    wavenum = jnp.tile(jnp.arange(mode_count, dtype=jnp.int32), 2)
    return (wavenum[None, :] <= levels_cut[:, None]).astype(jnp.float32)


def x_filter(columns, analysis_x, synthesis_x, keep_x):
    coeffs = (
        jnp.einsum("xk,czxj->czkj", analysis_x, columns, precision=highest)
        * keep_x[None, :, :, None]
    )
    return jnp.einsum("kx,czkj->czxj", synthesis_x, coeffs, precision=highest)


def on_device(velocity, cutoffs, plane_index, boundary_index):
    devices = lax.axis_size("slab")
    member_rows = velocity.shape[3]
    across = velocity.shape[4]
    along = member_rows * devices
    analysis_x, synthesis_x = basis_pair(along, KX)
    analysis_y, synthesis_y = basis_pair(across, KY)
    keep_x = mode_keep(cutoffs[0, 0], KX)
    keep_y = mode_keep(cutoffs[0, 1], KY)
    own_field = velocity[0]
    spectra = (
        jnp.einsum("czxy,yj->czxj", own_field, analysis_y, precision=highest)
        * keep_y[None, :, None, :]
    )
    columns = lax.all_to_all(spectra, "slab", split_axis=3, concat_axis=2, tiled=True)
    smooth = x_filter(columns, analysis_x, synthesis_x, keep_x)
    returned = lax.all_to_all(smooth, "slab", split_axis=2, concat_axis=3, tiled=True)
    result = jnp.einsum("czxj,jy->czxy", returned, synthesis_y, precision=highest)
    first_row = lax.axis_index("slab") * member_rows
    local_index = jnp.clip(plane_index[0] - first_row, 0, member_rows - 1)
    plane_part = lax.dynamic_index_in_dim(result, local_index, 2, keepdims=False)
    source_plane = spread(plane_part, "slab", plane_index[0] // member_rows)
    inflow = shifted(source_plane, "ens", 1)
    streamwise = first_row + jnp.arange(member_rows, dtype=jnp.int32)
    offset = jnp.abs(streamwise - boundary_index[0])
    distance = jnp.minimum(offset, along - offset)
    relax = jnp.exp(-distance.astype(jnp.float32) / (along / 4.0))
    weight = relax[None, None, :, None]
    blended = result + weight * (inflow[:, :, None, :] - result)
    return blended[None]


def solution(mesh):
    in_specs = (P("ens", None, None, "slab", None), P("ens", None, None), P("ens"), P("ens"))
    out_specs = P("ens", None, None, "slab", None)
    return jax.shard_map(
        on_device, mesh=mesh, in_specs=in_specs, out_specs=out_specs, check_vma=False
    )
```

profile of v0, /device:TPU:8, one launch (start us, length us, event | category | flops | bytes accessed | tf_op | source)
XLA Modules:
  0.0 1089.4 jit_solution(2496585179114449928)
XLA Ops:
  6.5 4.1 fusion.37
  10.7 0.8 slice_bitcast_fusion
  11.4 0.1 compare_convert_fusion.1
  11.5 84.5 %bitcast_multiply_fusion = f32[3,8,256,512]{2,3,1,0:T(8,128)} fusion(f32[8,512]{1,0:T(8,128)S(1)} %compare_convert_fusion.1, f32[1,3,8,256,1024]{4,3,2,1,0:T(8,128)} %param.4, f32[1024,256]{1,0:T(8,128)S(1)} %get-tuple-element.7, f32[1024,256]{1,0:T(8,128)S(1)} %get-tuple-element.8, f32[512]{0:T(512)S(1)} %pad_maximum_fusion.7), kind=kOutput, calls=%fused_computation.3 | convolution fusion | flops 38658899968 | bytes 39864320 | tf_op jit(solution)/shard_map/czxy,yj->czxj/dot_general | solution.py:59
  96.0 16.3 %copy.17 = f32[3,8,256,512]{2,1,0,3:T(8,128)} copy(f32[3,8,256,512]{2,3,1,0:T(8,128)} %bitcast_multiply_fusion) | data formatting | bytes 25165824 | tf_op jit(solution)/shard_map/mul | solution.py:59
  112.3 5.5 all-to-all-start
  117.9 0.1 compare_convert_fusion
  118.0 17.5 %fusion.27 = (f32[2048,512]{1,0:T(8,128)}, f32[2048,512]{1,0:T(8,128)}) fusion(), kind=kLoop, calls=%fused_computation.29 | loop fusion | flops 14680064 | bytes 8388608 | tf_op jit(solution)/shard_map/sin | solution.py:29
  135.6 252.6 %all-to-all-done = f32[3,8,256,512]{2,1,0,3:T(8,128)} async-done(((f32[3,8,256,512]{2,1,0,3:T(8,128)}), f32[3,8,256,512]{2,1,0,3:T(8,128)}, u32[]{:S(2)}, u32[]{:S(2)}) %all-to-all-start) | async-done | bytes 12582944 | tf_op jit(solution)/shard_map/all_to_all | solution.py:62
  388.1 16.6 %copy.36 = f32[3,8,256,8,64]{2,3,4,1,0:T(8,128)} copy(f32[3,8,256,8,64]{2,1,0,4,3:T(8,128)} %bitcast.4) | data formatting | bytes 25165824 | tf_op jit(solution)/shard_map/all_to_all | solution.py:62
  404.8 13.6 %all_to_all.29 = f32[3,8,2048,64]{2,3,1,0:T(8,128)} reshape(f32[3,8,8,256,64]{3,2,4,1,0:T(8,128)} %bitcast.77) | data formatting | bytes 25165824 | tf_op jit(solution)/shard_map/all_to_all | solution.py:62
  418.4 0.0 copy-start.1
  418.4 0.0 copy-start.2
  418.4 47.2 %fusion.4 = f32[3,8,64,1024]{3,2,1,0:T(8,128)} fusion(f32[3,8,2048,64]{2,3,1,0:T(8,128)} %all_to_all.29, f32[2048,512]{1,0:T(8,128)} %get-tuple-element.9, f32[2048,512]{1,0:T(8,128)} %get-tuple-element.10, f32[1024]{0:T(1024)S(1)} %pad_maximum_fusion.6), kind=kOutput, calls=%fused_computation.8 | convolution fusion | flops 38658899968 | bytes 27267072 | tf_op jit(solution)/shard_map/xk,czxj->czkj/dot_general | solution.py:42
  465.6 0.0 copy-done.1
  465.6 0.0 copy-done.2
  465.6 44.3 %fusion.9 = f32[3,8,2048,64]{2,3,1,0:T(8,128)} fusion(f32[2048,512]{1,0:T(8,128)S(1)} %copy-done.1, f32[2048,512]{1,0:T(8,128)S(1)} %copy-done.2, f32[3,8,64,1024]{3,2,1,0:T(8,128)} %fusion.4, f32[8,1024]{1,0:T(8,128)S(1)} %compare_convert_fusion), kind=kOutput, calls=%fused_computation.16 | convolution fusion | flops 38658375680 | bytes 27295744 | tf_op jit(solution)/shard_map/kx,czkj->czxj/dot_general | solution.py:45
  509.9 17.7 %copy.19 = f32[3,8,2048,64]{3,1,0,2:T(8,128)} copy(f32[3,8,2048,64]{2,3,1,0:T(8,128)} %fusion.9) | data formatting | bytes 25165824 | tf_op jit(solution)/shard_map/kx,czkj->czxj/transpose | solution.py:45
  527.6 20.5 %reshape.91 = f32[8,1,393216]{2,1,0:T(1,128)} reshape(f32[2048,3,8,64]{3,2,1,0:T(8,128)} %bitcast.74) | data formatting | bytes 25165824
  548.1 8.8 all-to-all-start.1
  556.9 0.0 all-reduce.2.cloned.1.call-start
  557.6 269.6 %all-to-all-done.1 = f32[8,1,393216]{2,1,0:T(1,128)} async-done(((f32[8,1,393216]{2,1,0:T(1,128)}), f32[8,1,393216]{2,1,0:T(1,128)}, u32[]{:S(2)}, u32[]{:S(2)}) %all-to-all-start.1) | async-done | bytes 12582944 | tf_op jit(solution)/shard_map/all_to_all | solution.py:64
  827.2 0.5 broadcast.88
  827.7 36.8 %reduce = f32[8,393216]{1,0:T(8,128)} reduce(f32[8,1,393216]{2,1,0:T(1,128)} %all-to-all-done.1, f32[]{:T(128)} %broadcast.88), dimensions={1}, to_apply=%all_to_all.30.reduce_sub_computation | reduce | bytes 25165828 | tf_op jit(solution)/shard_map/all_to_all | solution.py:64
  864.5 23.2 %reshape.92 = f32[2048,3,8,64]{3,2,1,0:T(8,128)} reshape(f32[8,393216]{1,0:T(8,128)} %reduce) | data formatting | bytes 25165824
  887.7 18.7 %copy.21 = f32[3,8,256,8,64]{2,4,3,1,0:T(8,128)} copy(f32[3,8,256,8,64]{4,1,0,2,3:T(8,128)} %bitcast.75) | data formatting | bytes 25165824 | tf_op jit(solution)/shard_map/all_to_all | solution.py:64
  906.4 85.2 %fusion.24 = f32[3,8,256,1024]{3,2,1,0:T(8,128)S(1)} fusion(f32[3,8,256,512]{2,3,1,0:T(8,128)} %bitcast.76, f32[1024,256]{1,0:T(8,128)S(1)} %get-tuple-element.7, f32[1024,256]{1,0:T(8,128)S(1)} %get-tuple-element.8), kind=kOutput, calls=%fused_computation.26 | convolution fusion | flops 38655229952 | bytes 39845888 | tf_op jit(solution)/shard_map/czxj,jy->czxy/dot_general | solution.py:65
  991.5 0.0 copy-start
  991.6 8.9 copy-done
  1000.5 0.1 broadcast_select_fusion
  1000.6 0.7 copy.37
  1001.2 0.0 all-reduce.2.cloned.1.call-update
  1001.9 55.8 %all-reduce.2.cloned.1.call-done = f32[3,8,1024]{2,1,0:T(8,128)} async-done(((f32[3,8,1024]{2,1,0:T(8,128)}), f32[3,8,1024]{2,1,0:T(8,128)}) %all-reduce.2.cloned.1.call-update) | async-done | bytes 98320 | tf_op jit(solution)/shard_map/psum | solution.py:14
  1057.7 1.5 collective-permute-start
  1059.2 4.2 collective-permute-done
  1063.4 18.8 %add_bitcast_fusion = f32[1,3,8,256,1024]{4,3,2,1,0:T(8,128)} fusion(f32[3,8,256,1024]{3,2,1,0:T(8,128)} %copy-done, f32[3,8,1024]{2,1,0:T(8,128)S(1)} %collective-permute-done, f32[256]{0:T(256)S(1)} %fusion.42), kind=kLoop, calls=%fused_computation.2 | loop fusion | flops 18874368 | bytes 50430976 | tf_op jit(solution)/shard_map/broadcast_in_dim | solution.py:77
  (9 shorter events, 0.1 us)
Async XLA Ops:
  112.3 275.8 %all-to-all-start = ((f32[3,8,256,512]{2,1,0,3:T(8,128)}), f32[3,8,256,512]{2,1,0,3:T(8,128)}, u32[]{:S(2)}, u32[]{:S(2)}) async-start(f32[3,8,256,512]{2,1,0,3:T(8,128)} %copy.17), calls=%async_computation | async-start | bytes 25165824 | tf_op jit(solution)/shard_map/all_to_all | solution.py:62
  418.4 47.2 %copy-start.1 = (f32[2048,512]{1,0:T(8,128)S(1)}, f32[2048,512]{1,0:T(8,128)}, u32[]{:S(2)}) copy-start(f32[2048,512]{1,0:T(8,128)} %get-tuple-element.9) | copy-start | bytes 12582916
  418.4 47.2 %copy-start.2 = (f32[2048,512]{1,0:T(8,128)S(1)}, f32[2048,512]{1,0:T(8,128)}, u32[]{:S(2)}) copy-start(f32[2048,512]{1,0:T(8,128)} %get-tuple-element.10) | copy-start | bytes 12582916
  548.1 279.1 %all-to-all-start.1 = ((f32[8,1,393216]{2,1,0:T(1,128)}), f32[8,1,393216]{2,1,0:T(1,128)}, u32[]{:S(2)}, u32[]{:S(2)}) async-start(f32[8,1,393216]{2,1,0:T(1,128)} %reshape.91), calls=%async_computation.1 | async-start | bytes 25165824 | tf_op jit(solution)/shard_map/all_to_all | solution.py:64
  556.9 500.8 %all-reduce.2.cloned.1.call-start = ((), (), s32[]{:S(2)}) async-start(), calls=%async_computation.2 | async-start | bytes 196608 | tf_op jit(solution)/shard_map/psum | solution.py:14
  991.5 8.9 copy-start
  1057.7 5.7 collective-permute-start
Sparse Core Ops, SparseCore 0:
  1001.4 56.2 all-reduce.1
where the time goes:
time: 1090 us
  waiting for transfers between devices  582 us (53%)
  matrix products  261 us (24%)
  local copies, waits for them, and re-layouts  138 us (13%)
  other arithmetic  77.5 us (7%)
  starting transfers between devices  15.8 us (1%)
  between operations  15.2 us (1%)
    all_to_all x1, waiting for transfers between devices, on_device(): lax.all_to_all(smooth, 'slab', split_axis=2, concat_axis=3, tiled=True)  270 us
    all_to_all x1, waiting for transfers between devices, on_device(): lax.all_to_all(spectra, 'slab', split_axis=3, concat_axis=2, tiled=True)  253 us
    dot_general x1, matrix products, on_device(): jnp.einsum('czxj,jy->czxy', returned, synthesis_y, precision=highest)  85.2 us
    dot_general x1, matrix products, on_device(): jnp.einsum('czxy,yj->czxj', own_field, analysis_y, precision=highest)  84.5 us
    psum x1, waiting for transfers between devices, spread(): return lax.psum(kept, axis)  55.8 us
    unnamed x13, local copies, waits for them, and re-layouts  53.3 us
    dot_general x1, matrix products, x_filter(): jnp.einsum('xk,czxj->czkj', analysis_x, columns, precision=highest)  47.2 us
    dot_general x1, matrix products, x_filter(): return jnp.einsum('kx,czkj->czxj', synthesis_x, coeffs, precision=highest)  44.3 us
  transfers between devices with their start and end apart: 4, of which 4 were waited for; matrix products, arithmetic and copies ran while one was open for 2% of the time, Pallas kernels for 0%

commit v1 on v0

--- a/solution.py
+++ b/solution.py
@@ -61,7 +61,10 @@
     )
     columns = lax.all_to_all(spectra, "slab", split_axis=3, concat_axis=2, tiled=True)
     smooth = x_filter(columns, analysis_x, synthesis_x, keep_x)
-    returned = lax.all_to_all(smooth, "slab", split_axis=2, concat_axis=3, tiled=True)
+    returned = jnp.concatenate(
+        lax.all_to_all(jnp.stack(jnp.split(smooth, lax.axis_size("slab"), axis=2)), "slab", 0, 0),
+        axis=3,
+    )
     result = jnp.einsum("czxj,jy->czxy", returned, synthesis_y, precision=highest)
     first_row = lax.axis_index("slab") * member_rows
     local_index = jnp.clip(plane_index[0] - first_row, 0, member_rows - 1)

time: 1090 us -> 999 us (0.917)
  local copies, waits for them, and re-layouts: 138 us -> 79.1 us
  other arithmetic: 77.5 us -> 40.7 us
    all_to_all x1 -> x0, other arithmetic: 36.8 us -> none  [on_device(): lax.all_to_all(smooth, 'slab', split_axis=2, concat_axis=3, tiled=True)]
    unnamed x13 -> x18, local copies, waits for them, and re-layouts: 53.3 us -> 18.8 us
    all_to_all x2 -> x0, local copies, waits for them, and re-layouts: 19.2 us -> none  [on_device(): lax.all_to_all(smooth, 'slab', split_axis=2, concat_axis=3, tiled=True)]
    transpose x1 -> x0, local copies, waits for them, and re-layouts: 17.7 us -> none  [x_filter(): return jnp.einsum('kx,czkj->czxj', synthesis_x, coeffs, precision=highest)]
    reshape x0 -> x1, local copies, waits for them, and re-layouts: none -> 11.5 us  [on_device(): jnp.concatenate(lax.all_to_all(jnp.stack(jnp.split(smooth, lax.axis_size(...]
where the time goes in v1:
time: 999 us; the launch traced here: 994 us
  waiting for transfers between devices  582 us (58%)
  matrix products  261 us (26%)
  local copies, waits for them, and re-layouts  79.1 us (8%)
  other arithmetic  40.7 us (4%)
  starting transfers between devices  15.8 us (2%)
  between operations  15 us (2%)
    all_to_all x1, waiting for transfers between devices, on_device(): lax.all_to_all(jnp.stack(jnp.split(smooth, lax.axis_size('slab'), axis=2)...  270 us
    all_to_all x1, waiting for transfers between devices, on_device(): lax.all_to_all(spectra, 'slab', split_axis=3, concat_axis=2, tiled=True)  253 us
    dot_general x1, matrix products, on_device(): jnp.einsum('czxj,jy->czxy', returned, synthesis_y, precision=highest)  85.1 us
    dot_general x1, matrix products, on_device(): jnp.einsum('czxy,yj->czxj', own_field, analysis_y, precision=highest)  84.4 us
    psum x1, waiting for transfers between devices, spread(): return lax.psum(kept, axis)  55.8 us
    dot_general x1, matrix products, x_filter(): jnp.einsum('xk,czxj->czkj', analysis_x, columns, precision=highest)  47.4 us
    dot_general x1, matrix products, x_filter(): return jnp.einsum('kx,czkj->czxj', synthesis_x, coeffs, precision=highest)  44.3 us
    all_to_all x2, local copies, waits for them, and re-layouts, on_device(): lax.all_to_all(spectra, 'slab', split_axis=3, concat_axis=2, tiled=True)  30.3 us
  transfers between devices with their start and end apart: 4, of which 4 were waited for; matrix products, arithmetic and copies ran while one was open for 2% of the time, Pallas kernels for 0%

profile of v1, /device:TPU:8, one launch (start us, length us, event | category | flops | bytes accessed | tf_op | source)
XLA Modules:
  0.0 994.1 jit_solution(18424202729167941049)
XLA Ops:
  6.5 4.1 fusion.45
  10.7 0.8 slice_bitcast_fusion.8
  11.4 0.1 compare_convert_fusion.1
  11.5 84.4 %bitcast_multiply_fusion = f32[3,8,256,512]{2,3,1,0:T(8,128)} fusion(f32[8,512]{1,0:T(8,128)S(1)} %compare_convert_fusion.1, f32[1,3,8,256,1024]{4,3,2,1,0:T(8,128)} %param.4, f32[1024,256]{1,0:T(8,128)S(1)} %get-tuple-element.7, f32[1024,256]{1,0:T(8,128)S(1)} %get-tuple-element.8, f32[512]{0:T(512)S(1)} %pad_maximum_fusion.7), kind=kOutput, calls=%fused_computation.3 | convolution fusion | flops 38658899968 | bytes 39864320 | tf_op jit(solution)/shard_map/czxy,yj->czxj/dot_general | solution.py:59
  95.9 16.3 %copy.11 = f32[3,8,256,512]{2,1,0,3:T(8,128)} copy(f32[3,8,256,512]{2,3,1,0:T(8,128)} %bitcast_multiply_fusion) | data formatting | bytes 25165824 | tf_op jit(solution)/shard_map/mul | solution.py:59
  112.2 5.6 all-to-all-start
  117.8 0.1 compare_convert_fusion
  117.9 17.5 %fusion.27 = (f32[2048,512]{1,0:T(8,128)}, f32[2048,512]{1,0:T(8,128)}) fusion(), kind=kLoop, calls=%fused_computation.29 | loop fusion | flops 14680064 | bytes 8388608 | tf_op jit(solution)/shard_map/sin | solution.py:29
  135.4 252.6 %all-to-all-done = f32[3,8,256,512]{2,1,0,3:T(8,128)} async-done(((f32[3,8,256,512]{2,1,0,3:T(8,128)}), f32[3,8,256,512]{2,1,0,3:T(8,128)}, u32[]{:S(2)}, u32[]{:S(2)}) %all-to-all-start) | async-done | bytes 12582944 | tf_op jit(solution)/shard_map/all_to_all | solution.py:62
  388.0 16.6 %copy.26 = f32[3,8,256,8,64]{2,3,4,1,0:T(8,128)} copy(f32[3,8,256,8,64]{2,1,0,4,3:T(8,128)} %bitcast.4) | data formatting | bytes 25165824 | tf_op jit(solution)/shard_map/all_to_all | solution.py:62
  404.7 13.6 %all_to_all.19 = f32[3,8,2048,64]{2,3,1,0:T(8,128)} reshape(f32[3,8,8,256,64]{3,2,4,1,0:T(8,128)} %bitcast.102) | data formatting | bytes 25165824 | tf_op jit(solution)/shard_map/all_to_all | solution.py:62
  418.3 0.0 copy-start.1
  418.3 0.0 copy-start.2
  418.3 47.4 %fusion.4 = f32[3,8,64,1024]{3,2,1,0:T(8,128)} fusion(f32[3,8,2048,64]{2,3,1,0:T(8,128)} %all_to_all.19, f32[2048,512]{1,0:T(8,128)} %get-tuple-element.9, f32[2048,512]{1,0:T(8,128)} %get-tuple-element.10, f32[1024]{0:T(1024)S(1)} %pad_maximum_fusion.6), kind=kOutput, calls=%fused_computation.8 | convolution fusion | flops 38658899968 | bytes 27267072 | tf_op jit(solution)/shard_map/xk,czxj->czkj/dot_general | solution.py:42
  465.7 0.0 copy-done.1
  465.7 0.0 copy-done.2
  465.7 44.3 %fusion.9 = f32[3,8,2048,64]{2,3,1,0:T(8,128)S(1)} fusion(f32[2048,512]{1,0:T(8,128)S(1)} %copy-done.1, f32[2048,512]{1,0:T(8,128)S(1)} %copy-done.2, f32[3,8,64,1024]{3,2,1,0:T(8,128)} %fusion.4, f32[8,1024]{1,0:T(8,128)S(1)} %compare_convert_fusion), kind=kOutput, calls=%fused_computation.16 | convolution fusion | flops 38658375680 | bytes 27295744 | tf_op jit(solution)/shard_map/kx,czkj->czxj/dot_general | solution.py:45
  510.1 1.3 fusion.37
  511.4 1.3 fusion.36
  512.7 1.3 fusion.35
  514.0 1.3 fusion.34
  515.4 1.3 fusion.33
  516.7 1.3 fusion.32
  518.0 1.3 fusion.31
  519.3 1.3 fusion.30
  520.6 8.8 all-to-all-start.1
  529.4 0.0 all-reduce.2.cloned.1.call-start
  530.1 269.6 %all-to-all-done.1 = f32[8,3,8,256,64]{3,4,2,1,0:T(8,128)} async-done(((f32[8,3,8,256,64]{3,4,2,1,0:T(8,128)}), f32[8,3,8,256,64]{3,4,2,1,0:T(8,128)}, u32[]{:S(2)}, u32[]{:S(2)}) %all-to-all-start.1) | async-done | bytes 12582944 | tf_op jit(solution)/shard_map/all_to_all | solution.py:65
  799.7 11.5 %copy.13 = f32[3,8,256,8,64]{2,4,3,1,0:T(8,128)} copy(f32[3,8,256,8,64]{2,4,1,0,3:T(8,128)} %bitcast.21) | data formatting | bytes 25165824 | tf_op jit(solution)/shard_map/reshape | solution.py:64
  811.2 85.1 %fusion.24 = f32[3,8,256,1024]{3,2,1,0:T(8,128)S(1)} fusion(f32[3,8,256,512]{2,3,1,0:T(8,128)} %bitcast.101, f32[1024,256]{1,0:T(8,128)S(1)} %get-tuple-element.7, f32[1024,256]{1,0:T(8,128)S(1)} %get-tuple-element.8), kind=kOutput, calls=%fused_computation.26 | convolution fusion | flops 38655229952 | bytes 39845888 | tf_op jit(solution)/shard_map/czxj,jy->czxy/dot_general | solution.py:68
  896.4 0.0 copy-start
  896.4 8.9 copy-done
  905.3 0.1 broadcast_select_fusion
  905.4 0.7 copy.27
  906.1 0.0 all-reduce.2.cloned.1.call-update
  906.7 55.8 %all-reduce.2.cloned.1.call-done = f32[3,8,1024]{2,1,0:T(8,128)} async-done(((f32[3,8,1024]{2,1,0:T(8,128)}), f32[3,8,1024]{2,1,0:T(8,128)}) %all-reduce.2.cloned.1.call-update) | async-done | bytes 98320 | tf_op jit(solution)/shard_map/psum | solution.py:14
  962.6 1.5 collective-permute-start
  964.0 4.2 collective-permute-done
  968.3 18.8 %add_bitcast_fusion = f32[1,3,8,256,1024]{4,3,2,1,0:T(8,128)} fusion(f32[3,8,256,1024]{3,2,1,0:T(8,128)} %copy-done, f32[3,8,1024]{2,1,0:T(8,128)S(1)} %collective-permute-done, f32[256]{0:T(256)S(1)} %fusion.50), kind=kLoop, calls=%fused_computation.2 | loop fusion | flops 18874368 | bytes 50430976 | tf_op jit(solution)/shard_map/broadcast_in_dim | solution.py:80
  (9 shorter events, 0.1 us)
Async XLA Ops:
  112.2 275.8 %all-to-all-start = ((f32[3,8,256,512]{2,1,0,3:T(8,128)}), f32[3,8,256,512]{2,1,0,3:T(8,128)}, u32[]{:S(2)}, u32[]{:S(2)}) async-start(f32[3,8,256,512]{2,1,0,3:T(8,128)} %copy.11), calls=%async_computation | async-start | bytes 25165824 | tf_op jit(solution)/shard_map/all_to_all | solution.py:62
  418.3 47.4 %copy-start.1 = (f32[2048,512]{1,0:T(8,128)S(1)}, f32[2048,512]{1,0:T(8,128)}, u32[]{:S(2)}) copy-start(f32[2048,512]{1,0:T(8,128)} %get-tuple-element.9) | copy-start | bytes 12582916
  418.3 47.4 %copy-start.2 = (f32[2048,512]{1,0:T(8,128)S(1)}, f32[2048,512]{1,0:T(8,128)}, u32[]{:S(2)}) copy-start(f32[2048,512]{1,0:T(8,128)} %get-tuple-element.10) | copy-start | bytes 12582916
  520.6 279.1 %all-to-all-start.1 = ((f32[8,3,8,256,64]{3,4,2,1,0:T(8,128)}), f32[8,3,8,256,64]{3,4,2,1,0:T(8,128)}, u32[]{:S(2)}, u32[]{:S(2)}) async-start(f32[8,3,8,256,64]{3,4,2,1,0:T(8,128)} %fusion.30), calls=%async_computation.1 | async-start | bytes 25165824 | tf_op jit(solution)/shard_map/all_to_all | solution.py:65
  529.4 433.1 %all-reduce.2.cloned.1.call-start = ((), (), s32[]{:S(2)}) async-start(), calls=%async_computation.2 | async-start | bytes 196608 | tf_op jit(solution)/shard_map/psum | solution.py:14
  896.4 8.9 copy-start
  962.6 5.7 collective-permute-start
Sparse Core Ops, SparseCore 0:
  906.2 56.2 all-reduce.1
